TPU v7x, 32 devices: a whole 2x2x4 slice. The times are simulated.
32 devices in a mesh: gx: 4 (over x, core), gy: 2 (over y), gz: 4 (over z).
Axes of the slice: x: 2, y: 2, z: 4, core: 2. Of those that a mesh axis runs over, the one named last changes fastest.
Arguments:
- fields: float32 [32, 32, 16, 512], P(None, 'gx', 'gy', 'gz'), may hold values from -8 to 8
- strength: float32 [32], replicated, may hold values from 0.3 to 1
Outputs:
- filtered: float32 [32, 32, 16, 512], P(None, 'gx', 'gy', 'gz')
All inputs are finite; a program needn't handle non-finite values.
Results may differ from a plain program's by a relative error of at most 0.00002.
Values sent between devices are 32-bit elements; how exact they have to be, the bound alone decides.
No kernel may reach another device: no remote copies, remote signals or barrier semaphores. Data moves between devices by JAX's collectives and lax.ppermute only.
A program may use at most 64 MiB of HBM per device.

v0:
```python
import jax
import jax.numpy as jnp
from jax import lax
from jax.sharding import PartitionSpec as P

filter_weights = [1.0, -10.0, 45.0, -120.0, 210.0, -252.0, 210.0, -120.0, 45.0, -10.0, 1.0]


def with_halo(cells, sides, width):
    for axis, dim in sides:
        count = lax.axis_size(axis)
        head = lax.slice_in_dim(cells, 0, width, axis=dim)
        tail = lax.slice_in_dim(cells, cells.shape[dim] - width, cells.shape[dim], axis=dim)
        cells = jnp.concatenate(
            [
                lax.ppermute(tail, axis, [(i, (i + 1) % count) for i in range(count)]),
                cells,
                lax.ppermute(head, axis, [((i + 1) % count, i) for i in range(count)]),
            ],
            axis=dim,
        )
    return cells


def difference_along(padded, axis, length, starts):
    total = None
    for index in range(11):
        begin = list(starts)
        begin[axis] = index
        piece = lax.slice_in_dim(padded, begin[axis], begin[axis] + length, axis=axis)
        term = filter_weights[index] * piece
        total = term if total is None else total + term
    return total


def local(fields, strength):
    cells_x = fields.shape[1]
    cells_y = fields.shape[2]
    cells_z = fields.shape[3]
    padded_x = with_halo(fields, (("gx", 1),), 5)
    summed = difference_along(padded_x, 1, cells_x, (0, 0, 0, 0))
    padded_y = with_halo(fields, (("gy", 2),), 5)
    summed = summed + difference_along(padded_y, 2, cells_y, (0, 0, 0, 0))
    padded_z = with_halo(fields, (("gz", 3),), 5)
    summed = summed + difference_along(padded_z, 3, cells_z, (0, 0, 0, 0))
    return fields + (strength / 1024.0)[:, None, None, None] * summed


def solution(mesh):
    return jax.shard_map(
        local,
        mesh=mesh,
        in_specs=(P(None, "gx", "gy", "gz"), P()),
        out_specs=P(None, "gx", "gy", "gz"),
        check_vma=False,
    )
```

profile of v0, /device:TPU:0, one launch (start us, length us, event | category | flops | bytes accessed | tf_op | source)
XLA Modules:
  0.0 53.8 jit_solution(14464115644586849275)
XLA Ops:
  0.0 1.7 %fusion.58 = (f32[32,8,5,128]{3,2,1,0:T(8,128)S(1)}, f32[32,8,5,128]{3,2,1,0:T(8,128)S(1)}) fusion(f32[32,8,8,128]{3,2,1,0:T(8,128)} %param.2), kind=kLoop, calls=%fused_computation.105 | loop fusion | bytes 2621440 | tf_op jit(solution)/shard_map/slice | solution.py:12
  1.7 0.0 copy-start
  1.7 1.0 %copy.11 = f32[32,8,5,128]{3,1,2,0:T(8,128)} copy(f32[32,8,5,128]{3,2,1,0:T(8,128)S(1)} %get-tuple-element.11) | data formatting | bytes 1310720
  2.7 3.0 %collective-permute-start.2 = (f32[32,8,5,128]{3,1,2,0:T(8,128)}, f32[32,8,5,128]{3,1,2,0:T(8,128)}, u32[]{:S(2)}, u32[]{:S(2)}) collective-permute-start(f32[32,8,5,128]{3,1,2,0:T(8,128)} %copy.11), channel_id=1, source_target_pairs={{0,4},{4,0},{1,5},{5,1},{2,6},{6,2},{3,7},{7,3},{8,12},{12,8},{9,1... | collective-permute-start | bytes 1966088 | tf_op jit(solution)/shard_map/ppermute | solution.py:16
  5.7 0.0 copy-done
  5.7 1.1 %fusion.57 = (f32[32,5,8,128]{3,2,1,0:T(8,128)}, f32[32,5,8,128]{3,2,1,0:T(8,128)}) fusion(f32[32,8,8,128]{3,2,1,0:T(8,128)S(1)} %copy-done), kind=kLoop, calls=%fused_computation.104 | loop fusion | bytes 2621440 | tf_op jit(solution)/shard_map/slice | solution.py:13
  6.8 0.0 collective-permute-start
  6.8 1.0 %copy.12 = f32[32,8,5,128]{3,1,2,0:T(8,128)} copy(f32[32,8,5,128]{3,2,1,0:T(8,128)S(1)} %get-tuple-element.10) | data formatting | bytes 1310720
  7.8 0.5 collective-permute-start.3
  8.3 0.4 fusion.59
  8.7 0.0 copy-start.3
  8.7 1.3 %copy.14 = f32[32,8,8,5]{0,2,3,1:T(8,128)} copy(f32[32,8,8,5]{3,2,1,0:T(8,128)S(1)} %get-tuple-element.13) | data formatting | bytes 81920
  10.0 3.6 %collective-permute-start.5 = (f32[32,8,8,5]{0,2,3,1:T(8,128)}, f32[32,8,8,5]{0,2,3,1:T(8,128)S(1)}, u32[]{:S(2)}, u32[]{:S(2)}) collective-permute-start(f32[32,8,8,5]{0,2,3,1:T(8,128)} %copy.14), channel_id=1, source_target_pairs={{1,0},{2,1},{3,2},{0,3},{5,4},{6,5},{7,6},{4,7},{9,8},{10,9},{11,1... | collective-permute-start | bytes 122888 | tf_op jit(solution)/shard_map/ppermute | solution.py:18
  13.7 1.2 %collective-permute-start.1 = (f32[32,5,8,128]{3,2,1,0:T(8,128)}, f32[32,5,8,128]{3,2,1,0:T(8,128)S(1)}, u32[]{:S(2)}, u32[]{:S(2)}) collective-permute-start(f32[32,5,8,128]{3,2,1,0:T(8,128)} %get-tuple-element.9), channel_id=1, source_target_pairs={{8,0},{16,8},{24,16},{0,24},{9,1},{17,9},{25,17},{1,25},{10,2},{18... | collective-permute-start | bytes 1966088 | tf_op jit(solution)/shard_map/ppermute | solution.py:18
  14.8 0.7 %copy.13 = f32[32,8,8,5]{0,2,3,1:T(8,128)S(1)} copy(f32[32,8,8,5]{3,2,1,0:T(8,128)S(1)} %get-tuple-element.12) | data formatting | bytes 81920
  15.5 2.7 %collective-permute-done.5 = f32[32,8,8,5]{0,2,3,1:T(8,128)S(1)} collective-permute-done((f32[32,8,8,5]{0,2,3,1:T(8,128)}, f32[32,8,8,5]{0,2,3,1:T(8,128)S(1)}, u32[]{:S(2)}, u32[]{:S(2)}) %collective-permute-start.5) | collective-permute-done | bytes 40992 | tf_op jit(solution)/shard_map/ppermute | solution.py:18
  18.2 0.4 collective-permute-start.4
  18.6 0.0 copy-done.3
  18.6 1.9 %copy.10 = f32[32,8,8,5]{3,2,1,0:T(8,128)} copy(f32[32,8,8,5]{0,2,3,1:T(8,128)S(1)} %collective-permute-done.5) | data formatting | bytes 81920 | tf_op jit(solution)/shard_map/ppermute | solution.py:18
  20.4 6.5 %collective-permute-done.4 = f32[32,8,8,5]{0,2,3,1:T(8,128)S(1)} collective-permute-done((f32[32,8,8,5]{0,2,3,1:T(8,128)S(1)}, f32[32,8,8,5]{0,2,3,1:T(8,128)S(1)}, u32[]{:S(2)}, u32[]{:S(2)}) %collective-permute-start.4) | collective-permute-done | bytes 40992 | tf_op jit(solution)/shard_map/ppermute | solution.py:16
  26.9 1.8 %copy.8 = f32[32,8,8,5]{3,2,1,0:T(8,128)} copy(f32[32,8,8,5]{0,2,3,1:T(8,128)S(1)} %collective-permute-done.4) | data formatting | bytes 81920 | tf_op jit(solution)/shard_map/ppermute | solution.py:16
  28.8 0.0 collective-permute-done.2
  28.8 2.3 %copy.4 = f32[32,8,5,128]{3,2,1,0:T(8,128)} copy(f32[32,8,5,128]{3,1,2,0:T(8,128)} %collective-permute-done.2) | data formatting | bytes 1310720 | tf_op jit(solution)/shard_map/ppermute | solution.py:16
  31.0 0.0 collective-permute-done
  31.0 1.1 %constant_dynamic-update-slice_fusion.1 = f32[32,13,8,128]{3,2,1,0:T(8,128)S(1)} fusion(f32[32,5,8,128]{3,2,1,0:T(8,128)} %collective-permute-done), kind=kLoop, calls=%fused_computation.99 | loop fusion | bytes 1310720
  32.2 0.2 constant_dynamic-update-slice_fusion
  32.4 0.0 copy-start.1
  32.4 2.4 %collective-permute-done.3 = f32[32,8,5,128]{3,1,2,0:T(8,128)} collective-permute-done((f32[32,8,5,128]{3,1,2,0:T(8,128)}, f32[32,8,5,128]{3,1,2,0:T(8,128)}, u32[]{:S(2)}, u32[]{:S(2)}) %collective-permute-start.3) | collective-permute-done | bytes 655392 | tf_op jit(solution)/shard_map/ppermute | solution.py:18
  34.8 1.3 %copy_dynamic-update-slice_fusion = f32[32,8,13,128]{3,2,1,0:T(8,128)S(1)} fusion(f32[32,8,13,128]{3,2,1,0:T(8,128)S(1)} %get-tuple-element.7, f32[32,8,5,128]{3,1,2,0:T(8,128)} %collective-permute-done.3), kind=kLoop, calls=%fused_computation.97 | loop fusion | bytes 1703936 | tf_op jit(solution)/shard_map/concatenate | solution.py:14
  36.1 0.0 copy-start.2
  36.1 0.0 collective-permute-done.1
  36.1 0.0 copy-done.1
  36.1 1.3 %copy-done.2 = f32[32,8,13,128]{3,2,1,0:T(8,128)} copy-done((f32[32,8,13,128]{3,2,1,0:T(8,128)}, f32[32,8,13,128]{3,2,1,0:T(8,128)S(1)}, u32[]{:S(2)}) %copy-start.2) | copy-done | bytes 1703960
  37.4 16.4 %fusion.6 = f32[32,8,8,128]{3,2,1,0:T(8,128)} fusion(f32[32,8,8,128]{3,2,1,0:T(8,128)S(1)} %copy-done, f32[32,8,8,5]{3,2,1,0:T(8,128)} %copy.10, f32[32,8,8,5]{3,2,1,0:T(8,128)} %copy.8, f32[32,8,5,128]{3,2,1,0:T(8,128)} %copy.4, f32[32,8,13,128]{3,2,1,0:T(8,128)} %copy-done.2, f32[32,13,8,128]{3,2,1,0:T(8,128)S(1)} %constant_dynamic-update-slice_fusion.2, ...), kind=kLoop, calls=%fused_computation.30 | loop fusion | flops 19398656 | bytes 18563200 | tf_op jit(solution)/shard_map/add | solution.py:46
  (2 shorter events, 0.0 us)
Async XLA Ops:
  1.7 4.0 %copy-start = (f32[32,8,8,128]{3,2,1,0:T(8,128)S(1)}, f32[32,8,8,128]{3,2,1,0:T(8,128)}, u32[]{:S(2)}) copy-start(f32[32,8,8,128]{3,2,1,0:T(8,128)} %param.2) | copy-start | bytes 3145732
  2.7 26.1 %collective-permute-start.2 = (f32[32,8,5,128]{3,1,2,0:T(8,128)}, f32[32,8,5,128]{3,1,2,0:T(8,128)}, u32[]{:S(2)}, u32[]{:S(2)}) collective-permute-start(f32[32,8,5,128]{3,1,2,0:T(8,128)} %copy.11), channel_id=1, source_target_pairs={{0,4},{4,0},{1,5},{5,1},{2,6},{6,2},{3,7},{7,3},{8,12},{12,8},{9,1... | collective-permute-start | bytes 1966088 | tf_op jit(solution)/shard_map/ppermute | solution.py:16
  6.8 24.2 %collective-permute-start = (f32[32,5,8,128]{3,2,1,0:T(8,128)}, f32[32,5,8,128]{3,2,1,0:T(8,128)}, u32[]{:S(2)}, u32[]{:S(2)}) collective-permute-start(f32[32,5,8,128]{3,2,1,0:T(8,128)} %get-tuple-element.8), channel_id=1, source_target_pairs={{0,8},{8,16},{16,24},{24,0},{1,9},{9,17},{17,25},{25,1},{2,10},{10... | collective-permute-start | bytes 1966088 | tf_op jit(solution)/shard_map/ppermute | solution.py:16
  7.8 26.9 %collective-permute-start.3 = (f32[32,8,5,128]{3,1,2,0:T(8,128)}, f32[32,8,5,128]{3,1,2,0:T(8,128)}, u32[]{:S(2)}, u32[]{:S(2)}) collective-permute-start(f32[32,8,5,128]{3,1,2,0:T(8,128)} %copy.12), channel_id=1, source_target_pairs={{4,0},{0,4},{5,1},{1,5},{6,2},{2,6},{7,3},{3,7},{12,8},{8,12},{13,... | collective-permute-start | bytes 1966088 | tf_op jit(solution)/shard_map/ppermute | solution.py:18
  8.7 9.8 %copy-start.3 = (f32[32]{0:T(128)S(1)}, f32[32]{0:T(128)}, u32[]{:S(2)}) copy-start(f32[32]{0:T(128)} %param.3) | copy-start | bytes 388
  10.0 8.2 %collective-permute-start.5 = (f32[32,8,8,5]{0,2,3,1:T(8,128)}, f32[32,8,8,5]{0,2,3,1:T(8,128)S(1)}, u32[]{:S(2)}, u32[]{:S(2)}) collective-permute-start(f32[32,8,8,5]{0,2,3,1:T(8,128)} %copy.14), channel_id=1, source_target_pairs={{1,0},{2,1},{3,2},{0,3},{5,4},{6,5},{7,6},{4,7},{9,8},{10,9},{11,1... | collective-permute-start | bytes 122888 | tf_op jit(solution)/shard_map/ppermute | solution.py:18
  13.7 22.4 %collective-permute-start.1 = (f32[32,5,8,128]{3,2,1,0:T(8,128)}, f32[32,5,8,128]{3,2,1,0:T(8,128)S(1)}, u32[]{:S(2)}, u32[]{:S(2)}) collective-permute-start(f32[32,5,8,128]{3,2,1,0:T(8,128)} %get-tuple-element.9), channel_id=1, source_target_pairs={{8,0},{16,8},{24,16},{0,24},{9,1},{17,9},{25,17},{1,25},{10,2},{18... | collective-permute-start | bytes 1966088 | tf_op jit(solution)/shard_map/ppermute | solution.py:18
  18.2 8.7 %collective-permute-start.4 = (f32[32,8,8,5]{0,2,3,1:T(8,128)S(1)}, f32[32,8,8,5]{0,2,3,1:T(8,128)S(1)}, u32[]{:S(2)}, u32[]{:S(2)}) collective-permute-start(f32[32,8,8,5]{0,2,3,1:T(8,128)S(1)} %copy.13), channel_id=1, source_target_pairs={{0,1},{1,2},{2,3},{3,0},{4,5},{5,6},{6,7},{7,4},{8,9},{9,10},{10,1... | collective-permute-start | bytes 122888 | tf_op jit(solution)/shard_map/ppermute | solution.py:16
  32.4 3.7 %copy-start.1 = (f32[32,13,8,128]{3,2,1,0:T(8,128)}, f32[32,13,8,128]{3,2,1,0:T(8,128)S(1)}, u32[]{:S(2)}) copy-start(f32[32,13,8,128]{3,2,1,0:T(8,128)S(1)} %get-tuple-element.5) | copy-start | bytes 5111812
  36.1 1.4 %copy-start.2 = (f32[32,8,13,128]{3,2,1,0:T(8,128)}, f32[32,8,13,128]{3,2,1,0:T(8,128)S(1)}, u32[]{:S(2)}) copy-start(f32[32,8,13,128]{3,2,1,0:T(8,128)S(1)} %copy_dynamic-update-slice_fusion) | copy-start | bytes 5111812
where the time goes:
time: 54.1 us; the launch traced here: 53.8 us
  local copies, waits for them, and re-layouts  17.1 us (32%)
  other arithmetic  16.4 us (30%)
  waiting for transfers between devices  11.6 us (21%)
  starting transfers between devices  8.64 us (16%)
    add x1, other arithmetic, local(): return fields + (strength / 1024.0)[:, None, None, None] * summed  16.4 us
    ppermute x3, waiting for transfers between devices, with_halo(): lax.ppermute(tail, axis, [(i, (i + 1) % count) for i in range(count)])  6.5 us
    unnamed x13, local copies, waits for them, and re-layouts  6.35 us
    ppermute x3, starting transfers between devices, with_halo(): lax.ppermute(head, axis, [((i + 1) % count, i) for i in range(count)])  5.29 us
    ppermute x3, waiting for transfers between devices, with_halo(): lax.ppermute(head, axis, [((i + 1) % count, i) for i in range(count)])  5.1 us
    ppermute x2, local copies, waits for them, and re-layouts, with_halo(): lax.ppermute(tail, axis, [(i, (i + 1) % count) for i in range(count)])  4.1 us
    ppermute x3, starting transfers between devices, with_halo(): lax.ppermute(tail, axis, [(i, (i + 1) % count) for i in range(count)])  3.35 us
    ppermute x1, local copies, waits for them, and re-layouts, with_halo(): lax.ppermute(head, axis, [((i + 1) % count, i) for i in range(count)])  1.86 us
  transfers between devices with their start and end apart: 6, of which 3 were waited for; matrix products, arithmetic and copies ran while one was open for 24% of the time, Pallas kernels for 0%

commit v1 on v0

v1 whole, which is shorter than its diff:
```python
import functools

import jax
import jax.numpy as jnp
import numpy as np
from jax import lax
from jax.experimental import pallas as pl
from jax.experimental.pallas import tpu as pltpu
from jax.sharding import PartitionSpec as P

WEIGHTS = (1.0, -10.0, 45.0, -120.0, 210.0, -252.0, 210.0, -120.0, 45.0, -10.0, 1.0)
HALF = 5
EDGE = 8
ANY = pl.BlockSpec(memory_space=pl.ANY)
SMEM = pl.BlockSpec(memory_space=pltpu.SMEM)


def band(rows, cols, offset):
    m = np.zeros((rows, cols), np.float32)
    for i in range(rows):
        for j in range(cols):
            d = offset + j - i
            if -HALF <= d <= HALF:
                m[i, j] = WEIGHTS[HALF + d]
    return m


def diagonals(matrix):
    n = matrix.shape[0]
    found = []
    for m in range(n):
        coef = np.array([matrix[i, (i + m) % n] for i in range(n)], np.float32)
        if np.any(coef):
            found.append((m, coef))
    return found


def column(values, cells, lanes):
    row = lax.broadcasted_iota(jnp.int32, (cells, lanes), 0)
    out = jnp.full((cells, lanes), float(values[0]), jnp.float32)
    for i in range(1, cells):
        if values[i] != values[i - 1]:
            out = jnp.where(row >= i, float(values[i]), out)
    return out


def along_y(block, diags):
    cells, lanes = block.shape[-2:]
    total = None
    for m, coef in diags:
        moved = block if m == 0 else pltpu.roll(block, (cells - m) % cells, block.ndim - 2)
        term = moved * column(coef, cells, lanes)
        total = term if total is None else total + term
    return total


def thirds(x):
    a = x.astype(jnp.bfloat16)
    rest = x - a.astype(jnp.float32)
    b = rest.astype(jnp.bfloat16)
    c = (rest - b.astype(jnp.float32)).astype(jnp.bfloat16)
    return a, b, c


def dot(a, b, dims):
    return lax.dot_general(a, b, (dims, ((), ())), preferred_element_type=jnp.float32)


def edges_kernel(pick_ref, u_ref, head_ref, tail_ref, low_ref, high_ref):
    block = u_ref[...]
    n, cx, cy, cz = block.shape
    head_ref[...] = block[:, :HALF]
    tail_ref[...] = block[:, cx - HALF:]
    rows = block.reshape(n * cx * cy, cz)
    edge = None
    for part in thirds(rows):
        term = dot(pick_ref[...], part, ((1,), (1,)))
        edge = term if edge is None else edge + term
    low_ref[...] = edge[:EDGE]
    high_ref[...] = edge[EDGE:]


def inner_kernel(own_y, scale_ref, band_ref, rim_ref, u_ref, before_ref, after_ref, low_ref, high_ref, out_ref):
    n, cx, cy, cz = u_ref.shape
    first = pl.program_id(0) * n
    rows = u_ref[...].reshape(n * cx * cy, cz)
    total = None
    for part in thirds(rows):
        term = dot(part, band_ref[...], ((1,), (0,)))
        total = term if total is None else total + term
    rim = jnp.concatenate([low_ref[...], high_ref[...]], axis=0)
    for part in thirds(rim):
        total = total + dot(part, rim_ref[...], ((0,), (0,)))
    total = total.reshape(n, cx, cy, cz)
    for s in range(n):
        planes = [before_ref[s, i] for i in range(HALF)] + [u_ref[s, i] for i in range(cx)]
        planes = planes + [after_ref[s, i] for i in range(HALF)]
        scale = scale_ref[first + s]
        for i in range(cx):
            here = planes[i + HALF]
            acc = WEIGHTS[HALF] * here
            for k in range(1, HALF + 1):
                acc = acc + WEIGHTS[HALF + k] * (planes[i + HALF - k] + planes[i + HALF + k])
            acc = acc + along_y(here, own_y) + total[s, i]
            out_ref[s, i] = here + scale * acc


def outer_kernel(sides, scale_ref, *refs):
    partial_ref, out_ref = refs[-2], refs[-1]
    n, cx = out_ref.shape[:2]
    first = pl.program_id(0) * n
    for s in range(n):
        scale = scale_ref[first + s]
        for i in range(cx):
            acc = None
            for ref, diags in zip(refs[:-2], sides):
                term = along_y(ref[s, i], diags)
                acc = term if acc is None else acc + term
            out_ref[s, i] = partial_ref[s, i] + scale * acc


def ring(axis, step):
    count = lax.axis_size(axis)
    return [(i, (i + step) % count) for i in range(count)]


def local(fields, strength):
    ns, cx, cy, cz = fields.shape
    block = 4
    grid = (ns // block,)
    rows = block * cx * cy
    f32 = jnp.float32

    def cells(width):
        return pl.BlockSpec((block, width, cy, cz), lambda b: (b, 0, 0, 0))

    whole = cells(cx)
    edge_spec = pl.BlockSpec((EDGE, rows), lambda b: (0, b))

    def fixed(a):
        return pl.BlockSpec(a.shape, lambda b: (0,) * a.ndim)

    def cost(flops, size):
        return pl.CostEstimate(flops=flops, bytes_accessed=size, transcendentals=0)

    if lax.axis_size("gy") == 2:
        other = lax.ppermute(fields, "gy", ring("gy", 1))
        y_in = [other]
        sides = [diagonals(band(cy, cy, -cy) + band(cy, cy, cy))]
    else:
        up = lax.ppermute(fields[:, :, cy - HALF:], "gy", ring("gy", 1))
        down = lax.ppermute(fields[:, :, :HALF], "gy", ring("gy", -1))
        gap = cy - HALF
        y_in = [jnp.pad(up, ((0, 0), (0, 0), (gap, 0), (0, 0))), jnp.pad(down, ((0, 0), (0, 0), (0, gap), (0, 0)))]
        sides = [diagonals(band(cy, cy, -cy)), diagonals(band(cy, cy, cy))]

    pick = np.zeros((2 * EDGE, cz), np.float32)
    rim = np.zeros((2 * EDGE, cz), np.float32)
    for i in range(HALF):
        pick[i, i] = 1.0
        pick[EDGE + i, cz - HALF + i] = 1.0
        for j in range(cz):
            for row, d in ((i, i - HALF - j), (EDGE + i, cz + i - j)):
                if -HALF <= d <= HALF:
                    rim[row, j] = WEIGHTS[HALF + d]
    pick = jnp.asarray(pick, jnp.bfloat16)
    rim = jnp.asarray(rim, jnp.bfloat16)
    band_z = jnp.asarray(band(cz, cz, 0), jnp.bfloat16)

    size = fields.size * 4
    head, tail, low, high = pl.pallas_call(
        edges_kernel,
        grid=grid,
        in_specs=[fixed(pick), whole],
        out_specs=[cells(HALF), cells(HALF), edge_spec, edge_spec],
        out_shape=[
            jax.ShapeDtypeStruct((ns, HALF, cy, cz), f32),
            jax.ShapeDtypeStruct((ns, HALF, cy, cz), f32),
            jax.ShapeDtypeStruct((EDGE, ns * cx * cy), f32),
            jax.ShapeDtypeStruct((EDGE, ns * cx * cy), f32),
        ],
        cost_estimate=cost(size, 2 * size),
        name="edges",
    )(pick, fields)
    before = lax.ppermute(tail, "gx", ring("gx", 1))
    after = lax.ppermute(head, "gx", ring("gx", -1))
    from_low = lax.ppermute(high, "gz", ring("gz", 1))
    from_high = lax.ppermute(low, "gz", ring("gz", -1))

    scale = strength / 1024.0
    partial = pl.pallas_call(
        functools.partial(inner_kernel, diagonals(band(cy, cy, 0))),
        grid=grid,
        in_specs=[SMEM, fixed(band_z), fixed(rim), whole, cells(HALF), cells(HALF), edge_spec, edge_spec],
        out_specs=whole,
        out_shape=jax.ShapeDtypeStruct(fields.shape, f32),
        cost_estimate=cost(20 * size, 3 * size),
        name="inner",
    )(scale, band_z, rim, fields, before, after, from_low, from_high)
    return pl.pallas_call(
        functools.partial(outer_kernel, sides),
        grid=grid,
        in_specs=[SMEM] + [whole] * (len(y_in) + 1),
        out_specs=whole,
        out_shape=jax.ShapeDtypeStruct(fields.shape, f32),
        cost_estimate=cost(5 * size, 3 * size),
        name="outer",
    )(scale, *y_in, partial)


def solution(mesh):
    return jax.shard_map(
        local,
        mesh=mesh,
        in_specs=(P(None, "gx", "gy", "gz"), P()),
        out_specs=P(None, "gx", "gy", "gz"),
        check_vma=False,
    )
```

time: 54.1 us -> 40.8 us (0.75)
  the two profiles are of different devices: /device:TPU:0 before, /device:TPU:1 now
where the time goes in v1:
time: 40.8 us; the launch traced here: 40.3 us
  Pallas kernels  18.5 us (45%)
  waiting for transfers between devices  11.8 us (29%)
  starting transfers between devices  7.49 us (18%)
  local copies, waits for them, and re-layouts  1.84 us (5%)
  other arithmetic  0.58 us (1%)
    ppermute x1, waiting for transfers between devices, local(): before = lax.ppermute(tail, 'gx', ring('gx', 1))  8.39 us
    pallas_call x1, Pallas kernels, local(): pl.pallas_call(functools.partial(inner_kernel, diagonals(band(cy, cy, 0))...  7 us
    pallas_call x1, Pallas kernels, local(): pl.pallas_call(functools.partial(outer_kernel, sides), grid=grid, in_spec...  5.85 us
    pallas_call x1, Pallas kernels, local(): pl.pallas_call(edges_kernel, grid=grid, in_specs=[fixed(pick), whole], ou...  5.69 us
    ppermute x1, starting transfers between devices, local(): from_high = lax.ppermute(low, 'gz', ring('gz', -1))  2.08 us
    ppermute x1, starting transfers between devices, local(): other = lax.ppermute(fields, 'gy', ring('gy', 1))  2.06 us
    ppermute x1, starting transfers between devices, local(): before = lax.ppermute(tail, 'gx', ring('gx', 1))  2.05 us
    unnamed x12, local copies, waits for them, and re-layouts  1.84 us
  transfers between devices with their start and end apart: 5, of which 4 were waited for; matrix products, arithmetic and copies ran while one was open for 1% of the time, Pallas kernels for 32%

profile of v1, /device:TPU:1, one launch (start us, length us, event | category | flops | bytes accessed | tf_op | source)
XLA Modules:
  0.0 40.3 jit_solution(3111763680403250715)
XLA Ops:
  0.0 2.1 %collective-permute-start = (f32[32,8,8,128]{3,2,1,0:T(8,128)}, f32[32,8,8,128]{3,2,1,0:T(8,128)S(1)}, u32[]{:S(2)}, u32[]{:S(2)}) collective-permute-start(f32[32,8,8,128]{3,2,1,0:T(8,128)} %u_ref.3), channel_id=1, source_target_pairs={{0,4},{4,0},{1,5},{5,1},{2,6},{6,2},{3,7},{7,3},{8,12},{12,8},{9,1... | collective-permute-start | bytes 3145736 | tf_op jit(solution)/shard_map/ppermute | solution.py:147
  2.1 5.7 %edges.1 = (f32[32,5,8,128]{3,2,1,0:T(8,128)}, f32[32,5,8,128]{3,2,1,0:T(8,128)}, f32[8,2048]{1,0:T(8,128)}, f32[8,2048]{1,0:T(8,128)}) custom-call(bf16[16,128]{1,0:T(8,128)(2,1)} %constant.9.clone.pick_ref, f32[32,8,8,128]{3,2,1,0:T(8,128)} %u_ref.3), custom_call_target="tpu_custom_call" | custom-call | flops 1048576 | bytes 2097152 | tf_op jit(solution)/shard_map/edges/pallas_call | solution.py:171
  7.8 2.1 %collective-permute-start.1 = (f32[32,5,8,128]{3,2,1,0:T(8,128)}, f32[32,5,8,128]{3,2,1,0:T(8,128)S(1)}, u32[]{:S(2)}, u32[]{:S(2)}) collective-permute-start(f32[32,5,8,128]{3,2,1,0:T(8,128)} %get-tuple-element.9), channel_id=1, source_target_pairs={{0,8},{8,16},{16,24},{24,0},{1,9},{9,17},{17,25},{25,1},{2,10},{10... | collective-permute-start | bytes 1966088 | tf_op jit(solution)/shard_map/ppermute | solution.py:185
  9.8 0.0 collective-permute-start.2
  9.8 0.0 copy-start.5
  9.8 1.3 %collective-permute-start.3 = (f32[8,2048]{1,0:T(8,128)}, f32[8,2048]{1,0:T(8,128)S(1)}, u32[]{:S(2)}, u32[]{:S(2)}) collective-permute-start(f32[8,2048]{1,0:T(8,128)} %get-tuple-element.11), channel_id=1, source_target_pairs={{0,1},{1,2},{2,3},{3,0},{4,5},{5,6},{6,7},{7,4},{8,9},{9,10},{10,1... | collective-permute-start | bytes 196616 | tf_op jit(solution)/shard_map/ppermute | solution.py:187
  11.1 2.1 %collective-permute-start.4 = (f32[8,2048]{1,0:T(8,128)}, f32[8,2048]{1,0:T(8,128)S(1)}, u32[]{:S(2)}, u32[]{:S(2)}) collective-permute-start(f32[8,2048]{1,0:T(8,128)} %get-tuple-element.12), channel_id=1, source_target_pairs={{0,3},{1,0},{2,1},{3,2},{4,7},{5,4},{6,5},{7,6},{8,11},{9,8},{10,9... | collective-permute-start | bytes 196616 | tf_op jit(solution)/shard_map/ppermute | solution.py:188
  13.2 0.0 copy-done.5
  13.2 0.6 %broadcast_multiply_fusion.scale_ref = f32[32]{0:T(128)} fusion(f32[32]{0:T(128)S(1)} %copy-done.5), kind=kLoop, calls=%fused_computation | loop fusion | flops 32 | bytes 256 | tf_op jit(solution)/shard_map/div | solution.py:190
  13.8 1.3 %collective-permute-done.3.low_ref = f32[8,2048]{1,0:T(8,128)S(1)} collective-permute-done((f32[8,2048]{1,0:T(8,128)}, f32[8,2048]{1,0:T(8,128)S(1)}, u32[]{:S(2)}, u32[]{:S(2)}) %collective-permute-start.3) | collective-permute-done | bytes 65568 | tf_op jit(solution)/shard_map/ppermute | solution.py:187
  15.1 0.0 copy-start.3
  15.1 0.3 collective-permute-done.4.high_ref
  15.4 0.0 copy-start.4
  15.4 8.4 %collective-permute-done.1.before_ref = f32[32,5,8,128]{3,2,1,0:T(8,128)S(1)} collective-permute-done((f32[32,5,8,128]{3,2,1,0:T(8,128)}, f32[32,5,8,128]{3,2,1,0:T(8,128)S(1)}, u32[]{:S(2)}, u32[]{:S(2)}) %collective-permute-start.1) | collective-permute-done | bytes 655392 | tf_op jit(solution)/shard_map/ppermute | solution.py:185
  23.8 0.0 copy-start.1
  23.8 1.7 %collective-permute-done.2.after_ref = f32[32,5,8,128]{3,2,1,0:T(8,128)S(1)} collective-permute-done((f32[32,5,8,128]{3,2,1,0:T(8,128)}, f32[32,5,8,128]{3,2,1,0:T(8,128)S(1)}, u32[]{:S(2)}, u32[]{:S(2)}) %collective-permute-start.2) | collective-permute-done | bytes 655392 | tf_op jit(solution)/shard_map/ppermute | solution.py:186
  25.6 0.0 copy-done.3
  25.6 0.0 copy-done.4
  25.6 0.0 copy-done.1
  25.6 0.0 copy-start.2
  25.6 0.8 %copy-done.2 = f32[32,5,8,128]{3,2,1,0:T(8,128)} copy-done((f32[32,5,8,128]{3,2,1,0:T(8,128)}, f32[32,5,8,128]{3,2,1,0:T(8,128)S(1)}, u32[]{:S(2)}) %copy-start.2) | copy-done | bytes 655384
  26.4 7.0 %inner.1.refs_1_ = f32[32,8,8,128]{3,2,1,0:T(8,128)} custom-call(f32[32]{0:T(128)} %broadcast_multiply_fusion.scale_ref, bf16[128,128]{1,0:T(8,128)(2,1)} %constant.11.clone.band_ref, bf16[16,128]{1,0:T(8,128)(2,1)} %constant.10.clone.rim_ref, f32[32,8,8,128]{3,2,1,0:T(8,128)} %u_ref.3, f32[32,5,8,128]{3,2,1,0:T(8,128)} %copy-done.1, ...), custom_call_target="tpu_custom_call" | custom-call | flops 20971520 | bytes 3145728 | tf_op jit(solution)/shard_map/inner/pallas_call | solution.py:191
  33.4 0.0 collective-permute-done.refs_0_
  33.4 0.0 copy-start
  33.4 1.0 %copy-done = f32[32,8,8,128]{3,2,1,0:T(8,128)} copy-done((f32[32,8,8,128]{3,2,1,0:T(8,128)}, f32[32,8,8,128]{3,2,1,0:T(8,128)S(1)}, u32[]{:S(2)}) %copy-start) | copy-done | bytes 1048600
  34.4 5.9 %outer.1 = f32[32,8,8,128]{3,2,1,0:T(8,128)} custom-call(f32[32]{0:T(128)} %broadcast_multiply_fusion.scale_ref, f32[32,8,8,128]{3,2,1,0:T(8,128)} %copy-done, f32[32,8,8,128]{3,2,1,0:T(8,128)} %inner.1.refs_1_), custom_call_target="tpu_custom_call" | custom-call | flops 5242880 | bytes 3145728 | tf_op jit(solution)/shard_map/outer/pallas_call | solution.py:200
Async XLA Ops:
  0.0 33.4 %collective-permute-start = (f32[32,8,8,128]{3,2,1,0:T(8,128)}, f32[32,8,8,128]{3,2,1,0:T(8,128)S(1)}, u32[]{:S(2)}, u32[]{:S(2)}) collective-permute-start(f32[32,8,8,128]{3,2,1,0:T(8,128)} %u_ref.3), channel_id=1, source_target_pairs={{0,4},{4,0},{1,5},{5,1},{2,6},{6,2},{3,7},{7,3},{8,12},{12,8},{9,1... | collective-permute-start | bytes 3145736 | tf_op jit(solution)/shard_map/ppermute | solution.py:147
  7.8 16.1 %collective-permute-start.1 = (f32[32,5,8,128]{3,2,1,0:T(8,128)}, f32[32,5,8,128]{3,2,1,0:T(8,128)S(1)}, u32[]{:S(2)}, u32[]{:S(2)}) collective-permute-start(f32[32,5,8,128]{3,2,1,0:T(8,128)} %get-tuple-element.9), channel_id=1, source_target_pairs={{0,8},{8,16},{16,24},{24,0},{1,9},{9,17},{17,25},{25,1},{2,10},{10... | collective-permute-start | bytes 1966088 | tf_op jit(solution)/shard_map/ppermute | solution.py:185
  9.8 15.8 %collective-permute-start.2 = (f32[32,5,8,128]{3,2,1,0:T(8,128)}, f32[32,5,8,128]{3,2,1,0:T(8,128)S(1)}, u32[]{:S(2)}, u32[]{:S(2)}) collective-permute-start(f32[32,5,8,128]{3,2,1,0:T(8,128)} %get-tuple-element.10), channel_id=1, source_target_pairs={{0,24},{8,0},{16,8},{24,16},{1,25},{9,1},{17,9},{25,17},{2,26},{10... | collective-permute-start | bytes 1966088 | tf_op jit(solution)/shard_map/ppermute | solution.py:186
  9.8 3.4 %copy-start.5 = (f32[32]{0:T(128)S(1)}, f32[32]{0:T(128)}, u32[]{:S(2)}) copy-start(f32[32]{0:T(128)} %param.6) | copy-start | bytes 388
  9.8 5.3 %collective-permute-start.3 = (f32[8,2048]{1,0:T(8,128)}, f32[8,2048]{1,0:T(8,128)S(1)}, u32[]{:S(2)}, u32[]{:S(2)}) collective-permute-start(f32[8,2048]{1,0:T(8,128)} %get-tuple-element.11), channel_id=1, source_target_pairs={{0,1},{1,2},{2,3},{3,0},{4,5},{5,6},{6,7},{7,4},{8,9},{9,10},{10,1... | collective-permute-start | bytes 196616 | tf_op jit(solution)/shard_map/ppermute | solution.py:187
  11.1 4.3 %collective-permute-start.4 = (f32[8,2048]{1,0:T(8,128)}, f32[8,2048]{1,0:T(8,128)S(1)}, u32[]{:S(2)}, u32[]{:S(2)}) collective-permute-start(f32[8,2048]{1,0:T(8,128)} %get-tuple-element.12), channel_id=1, source_target_pairs={{0,3},{1,0},{2,1},{3,2},{4,7},{5,4},{6,5},{7,6},{8,11},{9,8},{10,9... | collective-permute-start | bytes 196616 | tf_op jit(solution)/shard_map/ppermute | solution.py:188
  15.1 10.5 %copy-start.3 = (f32[8,2048]{1,0:T(8,128)}, f32[8,2048]{1,0:T(8,128)S(1)}, u32[]{:S(2)}) copy-start(f32[8,2048]{1,0:T(8,128)S(1)} %collective-permute-done.3.low_ref) | copy-start | bytes 196612
  15.4 10.1 %copy-start.4 = (f32[8,2048]{1,0:T(8,128)}, f32[8,2048]{1,0:T(8,128)S(1)}, u32[]{:S(2)}) copy-start(f32[8,2048]{1,0:T(8,128)S(1)} %collective-permute-done.4.high_ref) | copy-start | bytes 196612
  23.8 1.7 %copy-start.1 = (f32[32,5,8,128]{3,2,1,0:T(8,128)}, f32[32,5,8,128]{3,2,1,0:T(8,128)S(1)}, u32[]{:S(2)}) copy-start(f32[32,5,8,128]{3,2,1,0:T(8,128)S(1)} %collective-permute-done.1.before_ref) | copy-start | bytes 1966084
  25.6 0.8 %copy-start.2 = (f32[32,5,8,128]{3,2,1,0:T(8,128)}, f32[32,5,8,128]{3,2,1,0:T(8,128)S(1)}, u32[]{:S(2)}) copy-start(f32[32,5,8,128]{3,2,1,0:T(8,128)S(1)} %collective-permute-done.2.after_ref) | copy-start | bytes 1966084
  33.4 1.0 %copy-start = (f32[32,8,8,128]{3,2,1,0:T(8,128)}, f32[32,8,8,128]{3,2,1,0:T(8,128)S(1)}, u32[]{:S(2)}) copy-start(f32[32,8,8,128]{3,2,1,0:T(8,128)S(1)} %collective-permute-done.refs_0_) | copy-start | bytes 3145732

commit v2 on v0

v2 whole, which is shorter than its diff:
```python
import functools

import jax
import jax.numpy as jnp
import numpy as np
from jax import lax
from jax.experimental import pallas as pl
from jax.experimental.pallas import tpu as pltpu
from jax.sharding import PartitionSpec as P

WEIGHTS = (1.0, -10.0, 45.0, -120.0, 210.0, -252.0, 210.0, -120.0, 45.0, -10.0, 1.0)
HALF = 5
EDGE = 8
ANY = pl.BlockSpec(memory_space=pl.ANY)
SMEM = pl.BlockSpec(memory_space=pltpu.SMEM)
VMEM = pl.BlockSpec(memory_space=pltpu.VMEM)
HBM = pl.BlockSpec(memory_space=pltpu.HBM)
GRANT = 16 * 1024 * 1024


def band(rows, cols, offset):
    m = np.zeros((rows, cols), np.float32)
    for i in range(rows):
        for j in range(cols):
            d = offset + j - i
            if -HALF <= d <= HALF:
                m[i, j] = WEIGHTS[HALF + d]
    return m


def diagonals(matrix):
    n = matrix.shape[0]
    found = []
    for m in range(n):
        coef = np.array([matrix[i, (i + m) % n] for i in range(n)], np.float32)
        if np.any(coef):
            found.append((m, coef))
    return found


def column(values, cells, lanes):
    row = lax.broadcasted_iota(jnp.int32, (cells, lanes), 0)
    out = jnp.full((cells, lanes), float(values[0]), jnp.float32)
    for i in range(1, cells):
        if values[i] != values[i - 1]:
            out = jnp.where(row >= i, float(values[i]), out)
    return out


def along_y(block, diags):
    cells, lanes = block.shape[-2:]
    total = None
    for m, coef in diags:
        moved = block if m == 0 else pltpu.roll(block, (cells - m) % cells, block.ndim - 2)
        term = moved * (coef if coef.ndim == 2 else column(coef, cells, lanes))
        total = term if total is None else total + term
    return total


def thirds(x):
    a = x.astype(jnp.bfloat16)
    rest = x - a.astype(jnp.float32)
    b = rest.astype(jnp.bfloat16)
    c = (rest - b.astype(jnp.float32)).astype(jnp.bfloat16)
    return a, b, c


def dot(a, b, dims):
    return lax.dot_general(a, b, (dims, ((), ())), preferred_element_type=jnp.float32)


def slices_kernel(u_ref, head_ref, tail_ref, sems):
    cx = u_ref.shape[1]
    copies = [
        pltpu.make_async_copy(u_ref.at[:, pl.ds(cx - HALF, HALF)], tail_ref, sems.at[0]),
        pltpu.make_async_copy(u_ref.at[:, pl.ds(0, HALF)], head_ref, sems.at[1]),
    ]
    for copy in copies:
        copy.start()
    for copy in copies:
        copy.wait()


def edges_kernel(u_ref, low_ref, high_ref):
    ns, cx, cy, cz = u_ref.shape
    step = cz // (cx * cy)

    def body(b, carry):
        rows = u_ref[pl.ds(b * step, step)].reshape(cz, cz)
        turned = rows.T
        at = pl.ds(pl.multiple_of(b * cz, cz), cz)
        low_ref[:, at] = turned[:EDGE]
        high_ref[:, at] = turned[cz - EDGE:]
        return carry

    lax.fori_loop(0, ns // step, body, 0, unroll=2)


def inner_kernel(own_y, block, scale_ref, band_ref, rim_ref, u_ref, low_ref, high_ref, out_ref):
    ns, cx, cy, cz = u_ref.shape
    count = block * cx * cy

    def body(b, carry):
        u = u_ref[pl.ds(b * block, block)]
        rows = u.reshape(count, cz)
        at = pl.ds(pl.multiple_of(b * count, count), count)
        rim = jnp.concatenate(thirds(jnp.concatenate([low_ref[:, at], high_ref[:, at]], axis=0)), axis=0)
        total = dot(rim, rim_ref[...], ((0,), (0,)))
        total = total + dot(jnp.concatenate(thirds(rows), axis=1), band_ref[...], ((1,), (0,)))
        total = total.reshape(block, cx, cy, cz)
        for s in range(block):
            scale = scale_ref[b * block + s]
            for i in range(cx):
                here = u[s, i]
                out_ref[b * block + s, i] = here + scale * (along_y(here, own_y) + total[s, i])
        return carry

    lax.fori_loop(0, ns // block, body, 0)


def cross_kernel(scale_ref, u_ref, before_ref, after_ref, partial_ref, out_ref):
    ns, cx = u_ref.shape[:2]

    def body(s, carry):
        planes = [before_ref[s, i] for i in range(HALF)] + [u_ref[s, i] for i in range(cx)]
        planes = planes + [after_ref[s, i] for i in range(HALF)]
        scale = scale_ref[s]
        for i in range(cx):
            acc = WEIGHTS[HALF] * planes[i + HALF]
            for k in range(1, HALF + 1):
                acc = acc + WEIGHTS[HALF + k] * (planes[i + HALF - k] + planes[i + HALF + k])
            out_ref[s, i] = partial_ref[s, i] + scale * acc
        return carry

    lax.fori_loop(0, ns, body, 0)


def outer_kernel(sides, groups, scale_ref, *refs):
    partial_ref, out_ref, done_ref, sems = refs[-4:]
    ns, cx, cy, cz = partial_ref.shape
    size = ns // groups
    sides = [[(m, column(coef, cy, cz)) for m, coef in diags] for diags in sides]
    copies = []
    for g in range(groups):
        at = pl.ds(g * size, size)

        def body(s, carry):
            scale = scale_ref[s]
            for i in range(cx):
                acc = None
                for ref, diags in zip(refs[:-4], sides):
                    term = along_y(ref[s, i], diags)
                    acc = term if acc is None else acc + term
                done_ref[s, i] = partial_ref[s, i] + scale * acc
            return carry

        lax.fori_loop(g * size, (g + 1) * size, body, 0)
        copy = pltpu.make_async_copy(done_ref.at[at], out_ref.at[at], sems.at[g])
        copy.start()
        copies.append(copy)
    for copy in copies:
        copy.wait()


def ring(axis, step):
    count = lax.axis_size(axis)
    return [(i, (i + step) % count) for i in range(count)]


def local(fields, strength):
    ns, cx, cy, cz = fields.shape
    f32 = jnp.float32
    size = fields.size * 4

    def call(kernel, name, flops, out, n_in, scratch=(), scalars=1, in_space=VMEM, out_space=VMEM, **more):
        return pl.pallas_call(
            kernel,
            in_specs=[SMEM] * scalars + [in_space] * n_in,
            out_specs=[out_space] * len(out),
            out_shape=[jax.ShapeDtypeStruct(shape, f32) for shape in out],
            scratch_shapes=list(scratch),
            cost_estimate=pl.CostEstimate(flops=flops, bytes_accessed=size, transcendentals=0),
            compiler_params=pltpu.CompilerParams(vmem_limit_bytes=GRANT),
            name=name,
            **more,
        )

    if lax.axis_size("gy") == 2:
        y_in = [lax.ppermute(fields, "gy", ring("gy", 1))]
        sides = [diagonals(band(cy, cy, -cy) + band(cy, cy, cy))]
    else:
        up = lax.ppermute(fields[:, :, cy - HALF:], "gy", ring("gy", 1))
        down = lax.ppermute(fields[:, :, :HALF], "gy", ring("gy", -1))
        gap = cy - HALF
        y_in = [jnp.pad(up, ((0, 0), (0, 0), (gap, 0), (0, 0))), jnp.pad(down, ((0, 0), (0, 0), (0, gap), (0, 0)))]
        sides = [diagonals(band(cy, cy, -cy)), diagonals(band(cy, cy, cy))]

    layers = (ns, HALF, cy, cz)
    head, tail = call(
        slices_kernel, "slices", size, [layers] * 2, 1, [pltpu.SemaphoreType.DMA((2,))], scalars=0, in_space=HBM
    )(fields)
    before = lax.ppermute(tail, "gx", ring("gx", 1))
    after = lax.ppermute(head, "gx", ring("gx", -1))

    edge = (EDGE, ns * cx * cy)
    low, high = call(edges_kernel, "edges", size, [edge] * 2, 1, scalars=0)(fields)
    from_low = lax.ppermute(high, "gz", ring("gz", 1))
    from_high = lax.ppermute(low, "gz", ring("gz", -1))

    rim = np.zeros((2 * EDGE, cz), np.float32)
    for i in range(EDGE):
        for j in range(cz):
            for row, d in ((i, i - EDGE - j), (EDGE + i, cz + i - j)):
                if -HALF <= d <= HALF:
                    rim[row, j] = WEIGHTS[HALF + d]
    rim = jnp.asarray(np.tile(rim, (3, 1)), jnp.bfloat16)
    band_z = jnp.asarray(np.tile(band(cz, cz, 0), (3, 1)), jnp.bfloat16)

    scale = strength / 1024.0
    inner = functools.partial(inner_kernel, diagonals(band(cy, cy, 0)), 4)
    (partial,) = call(inner, "inner", 20 * size, [fields.shape], 5)(scale, band_z, rim, fields, from_low, from_high)
    (partial,) = call(cross_kernel, "cross", 5 * size, [fields.shape], 4, input_output_aliases={4: 0})(
        scale, fields, before, after, partial
    )
    groups = 4
    outer = functools.partial(outer_kernel, sides, groups)
    (out,) = call(
        outer,
        "outer",
        5 * size,
        [fields.shape],
        len(y_in) + 1,
        [pltpu.VMEM(fields.shape, f32), pltpu.SemaphoreType.DMA((groups,))],
        out_space=ANY,
    )(scale, *y_in, partial)
    return out


def solution(mesh):
    return jax.shard_map(
        local,
        mesh=mesh,
        in_specs=(P(None, "gx", "gy", "gz"), P()),
        out_specs=P(None, "gx", "gy", "gz"),
        check_vma=False,
    )
```

time: 54.1 us -> 28.8 us (0.53)
  other arithmetic: 16.4 us -> 0.01 us
  local copies, waits for them, and re-layouts: 17.1 us -> 1.27 us
  Pallas kernels: 0 us -> 7.27 us
    add x1 -> x0, other arithmetic: 16.4 us -> none  [local(): return fields + (strength / 1024.0)[:, None, None, None] * summed]
    pallas_call x0 -> x5, Pallas kernels: none -> 7.27 us  [the longest x1 2.5 us: local(): call(inner, 'inner', 20 * size, [fields.shape], 5)]
    ppermute x3 -> x0, local copies, waits for them, and re-layouts: 5.95 us -> none  [the longest x2 4.1 us: with_halo(): lax.ppermute(tail, axis, [(i, (i + 1) % count) for i in range(count)])]
    unnamed x13 -> x8, local copies, waits for them, and re-layouts: 6.35 us -> 1.27 us
    slice x3 -> x0, local copies, waits for them, and re-layouts: 3.22 us -> none  [the longest x1 1.72 us: with_halo(): head = lax.slice_in_dim(cells, 0, width, axis=dim)]
    concatenate x3 -> x0, local copies, waits for them, and re-layouts: 1.53 us -> none  [with_halo(): jnp.concatenate([lax.ppermute(tail, axis, [(i, (i + 1) % count) for i in...]
    ppermute x6 -> x5, waiting for transfers between devices: 11.6 us -> 11.3 us  [the longest x1 4.26 us: local(): y_in = [lax.ppermute(fields, 'gy', ring('gy', 1))]]
    ppermute x6 -> x5, starting transfers between devices: 8.64 us -> 8.65 us  [the longest x1 3 us: local(): y_in = [lax.ppermute(fields, 'gy', ring('gy', 1))]]
  transfers between devices with their start and end apart: 6 -> 5, of which waited for: 3 -> 5; matrix products, arithmetic and copies ran while one was open for 24% -> 0% of each run, Pallas kernels for 0% -> 18%
where the time goes in v2:
time: 28.8 us; the launch traced here: 28.6 us
  waiting for transfers between devices  11.3 us (39%)
  starting transfers between devices  8.65 us (30%)
  Pallas kernels  7.27 us (25%)
  local copies, waits for them, and re-layouts  1.27 us (4%)
    ppermute x1, waiting for transfers between devices, local(): y_in = [lax.ppermute(fields, 'gy', ring('gy', 1))]  4.26 us
    ppermute x1, waiting for transfers between devices, local(): before = lax.ppermute(tail, 'gx', ring('gx', 1))  3.55 us
    ppermute x1, starting transfers between devices, local(): y_in = [lax.ppermute(fields, 'gy', ring('gy', 1))]  3 us
    ppermute x1, waiting for transfers between devices, local(): from_low = lax.ppermute(high, 'gz', ring('gz', 1))  2.52 us
    pallas_call x1, Pallas kernels, local(): call(inner, 'inner', 20 * size, [fields.shape], 5)  2.5 us
    ppermute x1, starting transfers between devices, local(): from_high = lax.ppermute(low, 'gz', ring('gz', -1))  2.25 us
    pallas_call x1, Pallas kernels, local(): call(outer, 'outer', 5 * size, [fields.shape], len(y_in) + 1, [pltpu.VMEM...  2.24 us
    ppermute x1, starting transfers between devices, local(): after = lax.ppermute(head, 'gx', ring('gx', -1))  1.72 us
  transfers between devices with their start and end apart: 5, of which 5 were waited for; matrix products, arithmetic and copies ran while one was open for 0% of the time, Pallas kernels for 18%

profile of v2, /device:TPU:0, one launch (start us, length us, event | category | flops | bytes accessed | tf_op | source)
XLA Modules:
  0.0 28.6 jit_solution(1258839272559355379)
XLA Ops:
  0.0 3.0 %collective-permute-start = (f32[32,8,8,128]{3,2,1,0:T(8,128)}, f32[32,8,8,128]{3,2,1,0:T(8,128)S(1)}, u32[]{:S(2)}, u32[]{:S(2)}) collective-permute-start(f32[32,8,8,128]{3,2,1,0:T(8,128)} %u_ref.7), channel_id=1, source_target_pairs={{0,4},{4,0},{1,5},{5,1},{2,6},{6,2},{3,7},{7,3},{8,12},{12,8},{9,1... | collective-permute-start | bytes 3145736 | tf_op jit(solution)/shard_map/ppermute | solution.py:189
  3.0 0.0 copy-start
  3.0 1.3 %copy-done = f32[32,8,8,128]{3,2,1,0:T(8,128)S(1)} copy-done((f32[32,8,8,128]{3,2,1,0:T(8,128)S(1)}, f32[32,8,8,128]{3,2,1,0:T(8,128)}, u32[]{:S(2)}) %copy-start) | copy-done | bytes 1048600
  4.3 0.1 slices.1
  4.4 0.1 collective-permute-start.1
  4.5 0.0 copy-start.1
  4.5 1.7 %collective-permute-start.2 = (f32[32,5,8,128]{3,2,1,0:T(8,128)S(1)}, f32[32,5,8,128]{3,2,1,0:T(8,128)S(1)}, u32[]{:S(2)}, u32[]{:S(2)}) collective-permute-start(f32[32,5,8,128]{3,2,1,0:T(8,128)S(1)} %get-tuple-element.10), channel_id=1, source_target_pairs={{0,24},{8,0},{16,8},{24,16},{1,25},{9,1},{17,9},{25,17},{2,26},{10... | collective-permute-start | bytes 1966088 | tf_op jit(solution)/shard_map/ppermute | solution.py:203
  6.2 0.0 copy-start.2
  6.2 0.8 %edges.1 = (f32[8,2048]{1,0:T(8,128)S(1)}, f32[8,2048]{1,0:T(8,128)S(1)}) custom-call(f32[32,8,8,128]{3,2,1,0:T(8,128)S(1)} %copy-done), custom_call_target="tpu_custom_call" | custom-call | flops 1048576 | bytes 1048576 | tf_op jit(solution)/shard_map/edges/pallas_call | solution.py:206
  7.0 0.0 copy-start.3
  7.0 1.6 %collective-permute-start.3 = (f32[8,2048]{1,0:T(8,128)S(1)}, f32[8,2048]{1,0:T(8,128)S(1)}, u32[]{:S(2)}, u32[]{:S(2)}) collective-permute-start(f32[8,2048]{1,0:T(8,128)S(1)} %get-tuple-element.11), channel_id=1, source_target_pairs={{0,1},{1,2},{2,3},{3,0},{4,5},{5,6},{6,7},{7,4},{8,9},{9,10},{10,1... | collective-permute-start | bytes 196616 | tf_op jit(solution)/shard_map/ppermute | solution.py:207
  8.6 2.2 %collective-permute-start.4 = (f32[8,2048]{1,0:T(8,128)S(1)}, f32[8,2048]{1,0:T(8,128)S(1)}, u32[]{:S(2)}, u32[]{:S(2)}) collective-permute-start(f32[8,2048]{1,0:T(8,128)S(1)} %get-tuple-element.12), channel_id=1, source_target_pairs={{0,3},{1,0},{2,1},{3,2},{4,7},{5,4},{6,5},{7,6},{8,11},{9,8},{10,9... | collective-permute-start | bytes 196616 | tf_op jit(solution)/shard_map/ppermute | solution.py:208
  10.9 0.0 copy-done.3
  10.9 2.5 %collective-permute-done.3.low_ref = f32[8,2048]{1,0:T(8,128)S(1)} collective-permute-done((f32[8,2048]{1,0:T(8,128)S(1)}, f32[8,2048]{1,0:T(8,128)S(1)}, u32[]{:S(2)}, u32[]{:S(2)}) %collective-permute-start.3) | collective-permute-done | bytes 65568 | tf_op jit(solution)/shard_map/ppermute | solution.py:207
  13.4 0.2 collective-permute-done.4.high_ref
  13.6 0.0 copy-done.1
  13.6 0.0 copy-done.2
  13.6 2.5 %inner.1.partial_ref = f32[32,8,8,128]{3,2,1,0:T(8,128)S(1)} custom-call(f32[32]{0:T(128)S(1)} %broadcast_multiply_fusion.scale_ref, bf16[384,128]{1,0:T(8,128)(2,1)S(1)} %copy-done.1, bf16[48,128]{1,0:T(8,128)(2,1)S(1)} %copy-done.2, f32[32,8,8,128]{3,2,1,0:T(8,128)S(1)} %copy-done, f32[8,2048]{1,0:T(8,128)S(1)} %collective-permute-done.3.low_ref, ...), custom_call_target="tpu_custom_call" | custom-call | flops 20971520 | bytes 1048576 | tf_op jit(solution)/shard_map/inner/pallas_call | solution.py:221
  16.1 3.6 %collective-permute-done.1.before_ref = f32[32,5,8,128]{3,2,1,0:T(8,128)S(1)} collective-permute-done((f32[32,5,8,128]{3,2,1,0:T(8,128)S(1)}, f32[32,5,8,128]{3,2,1,0:T(8,128)S(1)}, u32[]{:S(2)}, u32[]{:S(2)}) %collective-permute-start.1) | collective-permute-done | bytes 655392 | tf_op jit(solution)/shard_map/ppermute | solution.py:202
  19.7 0.8 %collective-permute-done.2.after_ref = f32[32,5,8,128]{3,2,1,0:T(8,128)S(1)} collective-permute-done((f32[32,5,8,128]{3,2,1,0:T(8,128)S(1)}, f32[32,5,8,128]{3,2,1,0:T(8,128)S(1)}, u32[]{:S(2)}, u32[]{:S(2)}) %collective-permute-start.2) | collective-permute-done | bytes 655392 | tf_op jit(solution)/shard_map/ppermute | solution.py:203
  20.5 1.6 %cross.1.refs_1_ = f32[32,8,8,128]{3,2,1,0:T(8,128)S(1)} custom-call(f32[32]{0:T(128)S(1)} %broadcast_multiply_fusion.scale_ref, f32[32,8,8,128]{3,2,1,0:T(8,128)S(1)} %copy-done, f32[32,5,8,128]{3,2,1,0:T(8,128)S(1)} %collective-permute-done.1.before_ref, f32[32,5,8,128]{3,2,1,0:T(8,128)S(1)} %collective-permute-done.2.after_ref, ...), custom_call_target="tpu_custom_call", output_to_operand_aliasing={{}: (4, {})} | custom-call | flops 5242880 | bytes 1048576 | tf_op jit(solution)/shard_map/cross/pallas_call | solution.py:222
  22.1 4.3 %collective-permute-done.refs_0_ = f32[32,8,8,128]{3,2,1,0:T(8,128)S(1)} collective-permute-done((f32[32,8,8,128]{3,2,1,0:T(8,128)}, f32[32,8,8,128]{3,2,1,0:T(8,128)S(1)}, u32[]{:S(2)}, u32[]{:S(2)}) %collective-permute-start) | collective-permute-done | bytes 1048608 | tf_op jit(solution)/shard_map/ppermute | solution.py:189
  26.4 2.2 %outer.1 = f32[32,8,8,128]{3,2,1,0:T(8,128)} custom-call(f32[32]{0:T(128)S(1)} %broadcast_multiply_fusion.scale_ref, f32[32,8,8,128]{3,2,1,0:T(8,128)S(1)} %collective-permute-done.refs_0_, f32[32,8,8,128]{3,2,1,0:T(8,128)S(1)} %cross.1.refs_1_), custom_call_target="tpu_custom_call" | custom-call | flops 5242880 | bytes 1048576 | tf_op jit(solution)/shard_map/outer/pallas_call | solution.py:227
  (1 shorter events, 0.0 us)
Async XLA Ops:
  0.0 26.4 %collective-permute-start = (f32[32,8,8,128]{3,2,1,0:T(8,128)}, f32[32,8,8,128]{3,2,1,0:T(8,128)S(1)}, u32[]{:S(2)}, u32[]{:S(2)}) collective-permute-start(f32[32,8,8,128]{3,2,1,0:T(8,128)} %u_ref.7), channel_id=1, source_target_pairs={{0,4},{4,0},{1,5},{5,1},{2,6},{6,2},{3,7},{7,3},{8,12},{12,8},{9,1... | collective-permute-start | bytes 3145736 | tf_op jit(solution)/shard_map/ppermute | solution.py:189
  3.0 1.3 %copy-start = (f32[32,8,8,128]{3,2,1,0:T(8,128)S(1)}, f32[32,8,8,128]{3,2,1,0:T(8,128)}, u32[]{:S(2)}) copy-start(f32[32,8,8,128]{3,2,1,0:T(8,128)} %u_ref.7) | copy-start | bytes 3145732
  4.4 15.3 %collective-permute-start.1 = (f32[32,5,8,128]{3,2,1,0:T(8,128)S(1)}, f32[32,5,8,128]{3,2,1,0:T(8,128)S(1)}, u32[]{:S(2)}, u32[]{:S(2)}) collective-permute-start(f32[32,5,8,128]{3,2,1,0:T(8,128)S(1)} %get-tuple-element.9), channel_id=1, source_target_pairs={{0,8},{8,16},{16,24},{24,0},{1,9},{9,17},{17,25},{25,1},{2,10},{10... | collective-permute-start | bytes 1966088 | tf_op jit(solution)/shard_map/ppermute | solution.py:202
  4.5 9.2 %copy-start.1 = (bf16[384,128]{1,0:T(8,128)(2,1)S(1)}, bf16[384,128]{1,0:T(8,128)(2,1)}, u32[]{:S(2)}) copy-start(bf16[384,128]{1,0:T(8,128)(2,1)} %constant.8.clone.band_ref) | copy-start | bytes 294916
  4.5 16.0 %collective-permute-start.2 = (f32[32,5,8,128]{3,2,1,0:T(8,128)S(1)}, f32[32,5,8,128]{3,2,1,0:T(8,128)S(1)}, u32[]{:S(2)}, u32[]{:S(2)}) collective-permute-start(f32[32,5,8,128]{3,2,1,0:T(8,128)S(1)} %get-tuple-element.10), channel_id=1, source_target_pairs={{0,24},{8,0},{16,8},{24,16},{1,25},{9,1},{17,9},{25,17},{2,26},{10... | collective-permute-start | bytes 1966088 | tf_op jit(solution)/shard_map/ppermute | solution.py:203
  6.2 7.4 %copy-start.2 = (bf16[48,128]{1,0:T(8,128)(2,1)S(1)}, bf16[48,128]{1,0:T(8,128)(2,1)}, u32[]{:S(2)}) copy-start(bf16[48,128]{1,0:T(8,128)(2,1)} %constant.7.clone.rim_ref) | copy-start | bytes 36868
  7.0 3.9 %copy-start.3 = (f32[32]{0:T(128)S(1)}, f32[32]{0:T(128)}, u32[]{:S(2)}) copy-start(f32[32]{0:T(128)} %param.5) | copy-start | bytes 388
  7.0 6.4 %collective-permute-start.3 = (f32[8,2048]{1,0:T(8,128)S(1)}, f32[8,2048]{1,0:T(8,128)S(1)}, u32[]{:S(2)}, u32[]{:S(2)}) collective-permute-start(f32[8,2048]{1,0:T(8,128)S(1)} %get-tuple-element.11), channel_id=1, source_target_pairs={{0,1},{1,2},{2,3},{3,0},{4,5},{5,6},{6,7},{7,4},{8,9},{9,10},{10,1... | collective-permute-start | bytes 196616 | tf_op jit(solution)/shard_map/ppermute | solution.py:207
  8.6 5.0 %collective-permute-start.4 = (f32[8,2048]{1,0:T(8,128)S(1)}, f32[8,2048]{1,0:T(8,128)S(1)}, u32[]{:S(2)}, u32[]{:S(2)}) collective-permute-start(f32[8,2048]{1,0:T(8,128)S(1)} %get-tuple-element.12), channel_id=1, source_target_pairs={{0,3},{1,0},{2,1},{3,2},{4,7},{5,4},{6,5},{7,6},{8,11},{9,8},{10,9... | collective-permute-start | bytes 196616 | tf_op jit(solution)/shard_map/ppermute | solution.py:208

commit v3 on v2

--- a/solution.py
+++ b/solution.py
@@ -15,6 +15,8 @@
 SMEM = pl.BlockSpec(memory_space=pltpu.SMEM)
 VMEM = pl.BlockSpec(memory_space=pltpu.VMEM)
 HBM = pl.BlockSpec(memory_space=pltpu.HBM)
+GROUPS = (12, 20, 28)
+UNROLL = 4
 GRANT = 16 * 1024 * 1024
 
 
@@ -28,32 +30,54 @@
     return m
 
 
-def diagonals(matrix):
+def terms(matrix):
     n = matrix.shape[0]
+    left = matrix.copy()
     found = []
     for m in range(n):
-        coef = np.array([matrix[i, (i + m) % n] for i in range(n)], np.float32)
-        if np.any(coef):
-            found.append((m, coef))
+        at = (np.arange(n), (np.arange(n) + m) % n)
+        if np.count_nonzero(left[at]) > n // 2:
+            found.append((at[1], left[at].copy()))
+            left[at] = 0.0
+    while np.any(left):
+        source, coef = np.arange(n), np.zeros(n, np.float32)
+        for i in range(n):
+            if np.any(left[i]):
+                source[i] = np.flatnonzero(left[i])[0]
+                coef[i] = left[i, source[i]]
+                left[i, source[i]] = 0.0
+        found.append((source, coef))
     return found
 
 
-def column(values, cells, lanes):
+def column(values, cells, lanes, kind):
     row = lax.broadcasted_iota(jnp.int32, (cells, lanes), 0)
-    out = jnp.full((cells, lanes), float(values[0]), jnp.float32)
+    out = jnp.full((cells, lanes), values[0].item(), kind)
     for i in range(1, cells):
         if values[i] != values[i - 1]:
-            out = jnp.where(row >= i, float(values[i]), out)
+            out = jnp.where(row >= i, values[i].item(), out)
     return out
 
 
-def along_y(block, diags):
-    cells, lanes = block.shape[-2:]
+def prepared(rows, cells, lanes):
+    out = []
+    for source, coef in rows:
+        shift = int(source[0])
+        if not np.array_equal(source, (np.arange(cells) + shift) % cells):
+            shift = column(source, cells, lanes, jnp.int32)
+        out.append((shift, column(coef, cells, lanes, jnp.float32)))
+    return out
+
+
+def along_y(block, rows):
+    cells = block.shape[0]
     total = None
-    for m, coef in diags:
-        moved = block if m == 0 else pltpu.roll(block, (cells - m) % cells, block.ndim - 2)
-        term = moved * (coef if coef.ndim == 2 else column(coef, cells, lanes))
-        total = term if total is None else total + term
+    for shift, coef in rows:
+        if not isinstance(shift, int):
+            moved = jnp.take_along_axis(block, shift, axis=0, mode="promise_in_bounds")
+        else:
+            moved = pltpu.roll(block, cells - shift, 0) if shift else block
+        total = moved * coef if total is None else total + moved * coef
     return total
 
 
@@ -99,6 +123,7 @@
 def inner_kernel(own_y, block, scale_ref, band_ref, rim_ref, u_ref, low_ref, high_ref, out_ref):
     ns, cx, cy, cz = u_ref.shape
     count = block * cx * cy
+    own_y = prepared(own_y, cy, cz)
 
     def body(b, carry):
         u = u_ref[pl.ds(b * block, block)]
@@ -109,7 +134,7 @@
         total = total + dot(jnp.concatenate(thirds(rows), axis=1), band_ref[...], ((1,), (0,)))
         total = total.reshape(block, cx, cy, cz)
         for s in range(block):
-            scale = scale_ref[b * block + s]
+            scale = scale_ref[pl.ds(b * block + s, 1), :]
             for i in range(cx):
                 here = u[s, i]
                 out_ref[b * block + s, i] = here + scale * (along_y(here, own_y) + total[s, i])
@@ -124,7 +149,7 @@
     def body(s, carry):
         planes = [before_ref[s, i] for i in range(HALF)] + [u_ref[s, i] for i in range(cx)]
         planes = planes + [after_ref[s, i] for i in range(HALF)]
-        scale = scale_ref[s]
+        scale = scale_ref[pl.ds(s, 1), :]
         for i in range(cx):
             acc = WEIGHTS[HALF] * planes[i + HALF]
             for k in range(1, HALF + 1):
@@ -135,26 +160,26 @@
     lax.fori_loop(0, ns, body, 0)
 
 
-def outer_kernel(sides, groups, scale_ref, *refs):
-    partial_ref, out_ref, done_ref, sems = refs[-4:]
-    ns, cx, cy, cz = partial_ref.shape
-    size = ns // groups
-    sides = [[(m, column(coef, cy, cz)) for m, coef in diags] for diags in sides]
+def outer_kernel(sides, cuts, scale_ref, partial_ref, *refs):
+    y_refs = refs[:-3]
+    out_ref, done_ref, sems = refs[-3:]
+    cx, cy, cz = partial_ref.shape[1:]
+    sides = [prepared(rows, cy, cz) for rows in sides]
     copies = []
-    for g in range(groups):
-        at = pl.ds(g * size, size)
+    for g, (low, high) in enumerate(zip(cuts[:-1], cuts[1:])):
 
         def body(s, carry):
-            scale = scale_ref[s]
+            scale = scale_ref[pl.ds(s, 1), :]
             for i in range(cx):
                 acc = None
-                for ref, diags in zip(refs[:-4], sides):
-                    term = along_y(ref[s, i], diags)
+                for ref, rows in zip(y_refs, sides):
+                    term = along_y(ref[s, i], rows)
                     acc = term if acc is None else acc + term
                 done_ref[s, i] = partial_ref[s, i] + scale * acc
             return carry
 
-        lax.fori_loop(g * size, (g + 1) * size, body, 0)
+        lax.fori_loop(low, high, body, 0, unroll=UNROLL)
+        at = pl.ds(low, high - low)
         copy = pltpu.make_async_copy(done_ref.at[at], out_ref.at[at], sems.at[g])
         copy.start()
         copies.append(copy)
@@ -172,10 +197,10 @@
     f32 = jnp.float32
     size = fields.size * 4
 
-    def call(kernel, name, flops, out, n_in, scratch=(), scalars=1, in_space=VMEM, out_space=VMEM, **more):
+    def call(kernel, name, flops, out, n_in, scratch=(), in_space=VMEM, out_space=VMEM, **more):
         return pl.pallas_call(
             kernel,
-            in_specs=[SMEM] * scalars + [in_space] * n_in,
+            in_specs=in_space if isinstance(in_space, list) else [in_space] * n_in,
             out_specs=[out_space] * len(out),
             out_shape=[jax.ShapeDtypeStruct(shape, f32) for shape in out],
             scratch_shapes=list(scratch),
@@ -187,23 +212,23 @@
 
     if lax.axis_size("gy") == 2:
         y_in = [lax.ppermute(fields, "gy", ring("gy", 1))]
-        sides = [diagonals(band(cy, cy, -cy) + band(cy, cy, cy))]
+        sides = [terms(band(cy, cy, -cy) + band(cy, cy, cy))]
     else:
         up = lax.ppermute(fields[:, :, cy - HALF:], "gy", ring("gy", 1))
         down = lax.ppermute(fields[:, :, :HALF], "gy", ring("gy", -1))
         gap = cy - HALF
         y_in = [jnp.pad(up, ((0, 0), (0, 0), (gap, 0), (0, 0))), jnp.pad(down, ((0, 0), (0, 0), (0, gap), (0, 0)))]
-        sides = [diagonals(band(cy, cy, -cy)), diagonals(band(cy, cy, cy))]
+        sides = [terms(band(cy, cy, -cy)), terms(band(cy, cy, cy))]
 
     layers = (ns, HALF, cy, cz)
     head, tail = call(
-        slices_kernel, "slices", size, [layers] * 2, 1, [pltpu.SemaphoreType.DMA((2,))], scalars=0, in_space=HBM
+        slices_kernel, "slices", size, [layers] * 2, 1, [pltpu.SemaphoreType.DMA((2,))], in_space=HBM
     )(fields)
     before = lax.ppermute(tail, "gx", ring("gx", 1))
     after = lax.ppermute(head, "gx", ring("gx", -1))
 
     edge = (EDGE, ns * cx * cy)
-    low, high = call(edges_kernel, "edges", size, [edge] * 2, 1, scalars=0)(fields)
+    low, high = call(edges_kernel, "edges", size, [edge] * 2, 1)(fields)
     from_low = lax.ppermute(high, "gz", ring("gz", 1))
     from_high = lax.ppermute(low, "gz", ring("gz", -1))
 
@@ -216,23 +241,23 @@
     rim = jnp.asarray(np.tile(rim, (3, 1)), jnp.bfloat16)
     band_z = jnp.asarray(np.tile(band(cz, cz, 0), (3, 1)), jnp.bfloat16)
 
-    scale = strength / 1024.0
-    inner = functools.partial(inner_kernel, diagonals(band(cy, cy, 0)), 4)
-    (partial,) = call(inner, "inner", 20 * size, [fields.shape], 5)(scale, band_z, rim, fields, from_low, from_high)
-    (partial,) = call(cross_kernel, "cross", 5 * size, [fields.shape], 4, input_output_aliases={4: 0})(
+    scale = jnp.broadcast_to((strength / 1024.0)[:, None], (ns, cz))
+    inner = functools.partial(inner_kernel, terms(band(cy, cy, 0)), 4)
+    (partial,) = call(inner, "inner", 20 * size, [fields.shape], 6)(scale, band_z, rim, fields, from_low, from_high)
+    (partial,) = call(cross_kernel, "cross", 5 * size, [fields.shape], 5, input_output_aliases={4: 0})(
         scale, fields, before, after, partial
     )
-    groups = 4
-    outer = functools.partial(outer_kernel, sides, groups)
+    cuts = [0] + sorted({ns * c // 32 for c in GROUPS} - {0, ns}) + [ns]
+    outer = functools.partial(outer_kernel, sides, cuts)
     (out,) = call(
         outer,
         "outer",
         5 * size,
         [fields.shape],
-        len(y_in) + 1,
-        [pltpu.VMEM(fields.shape, f32), pltpu.SemaphoreType.DMA((groups,))],
-        out_space=ANY,
-    )(scale, *y_in, partial)
+        2 + len(y_in),
+        [pltpu.VMEM(fields.shape, f32), pltpu.SemaphoreType.DMA((len(cuts) - 1,))],
+        out_space=HBM,
+    )(scale, partial, *y_in)
     return out
 
 

time: 28.8 us -> 27.8 us (0.965)
  Pallas kernels: 7.27 us -> 5.24 us
  waiting for transfers between devices: 11.3 us -> 12.4 us
    pallas_call x4, Pallas kernels: 7.14 us -> 5.11 us  [the longest x1 1.96 us: local(): call(inner, 'inner', 20 * size, [fields.shape], 6)]
    ppermute x1, waiting for transfers between devices: 4.26 us -> 4.8 us  [local(): y_in = [lax.ppermute(fields, 'gy', ring('gy', 1))]]
    ppermute x1, waiting for transfers between devices: 3.55 us -> 4.03 us  [local(): before = lax.ppermute(tail, 'gx', ring('gx', 1))]
  transfers between devices with their start and end apart: 5 -> 5, of which waited for: 5 -> 5; matrix products, arithmetic and copies ran while one was open for 0% -> 0% of each run, Pallas kernels for 18% -> 14%
where the time goes in v3:
time: 27.8 us; the launch traced here: 27.7 us
  waiting for transfers between devices  12.4 us (45%)
  starting transfers between devices  8.65 us (31%)
  Pallas kernels  5.24 us (19%)
  local copies, waits for them, and re-layouts  1.34 us (5%)
    ppermute x1, waiting for transfers between devices, local(): y_in = [lax.ppermute(fields, 'gy', ring('gy', 1))]  4.8 us
    ppermute x1, waiting for transfers between devices, local(): before = lax.ppermute(tail, 'gx', ring('gx', 1))  4.03 us
    ppermute x1, starting transfers between devices, local(): y_in = [lax.ppermute(fields, 'gy', ring('gy', 1))]  3 us
    ppermute x1, waiting for transfers between devices, local(): from_low = lax.ppermute(high, 'gz', ring('gz', 1))  2.52 us
    ppermute x1, starting transfers between devices, local(): from_high = lax.ppermute(low, 'gz', ring('gz', -1))  2.25 us
    pallas_call x1, Pallas kernels, local(): call(inner, 'inner', 20 * size, [fields.shape], 6)  1.96 us
    ppermute x1, starting transfers between devices, local(): after = lax.ppermute(head, 'gx', ring('gx', -1))  1.72 us
    ppermute x1, starting transfers between devices, local(): from_low = lax.ppermute(high, 'gz', ring('gz', 1))  1.63 us
  transfers between devices with their start and end apart: 5, of which 5 were waited for; matrix products, arithmetic and copies ran while one was open for 0% of the time, Pallas kernels for 14%

profile of v3, /device:TPU:0, one launch (start us, length us, event | category | flops | bytes accessed | tf_op | source)
XLA Modules:
  0.0 27.7 jit_solution(7378843639386700063)
XLA Ops:
  0.0 3.0 %collective-permute-start.4 = (f32[32,8,8,128]{3,2,1,0:T(8,128)}, f32[32,8,8,128]{3,2,1,0:T(8,128)S(1)}, u32[]{:S(2)}, u32[]{:S(2)}) collective-permute-start(f32[32,8,8,128]{3,2,1,0:T(8,128)} %u_ref.7), channel_id=1, source_target_pairs={{0,4},{4,0},{1,5},{5,1},{2,6},{6,2},{3,7},{7,3},{8,12},{12,8},{9,1... | collective-permute-start | bytes 3145736 | tf_op jit(solution)/shard_map/ppermute | solution.py:214
  3.0 0.0 copy-start
  3.0 1.3 %copy-done = f32[32,8,8,128]{3,2,1,0:T(8,128)S(1)} copy-done((f32[32,8,8,128]{3,2,1,0:T(8,128)S(1)}, f32[32,8,8,128]{3,2,1,0:T(8,128)}, u32[]{:S(2)}) %copy-start) | copy-done | bytes 1048600
  4.3 0.1 slices.1
  4.4 0.1 collective-permute-start
  4.5 0.0 copy-start.1
  4.5 1.7 %collective-permute-start.1 = (f32[32,5,8,128]{3,2,1,0:T(8,128)S(1)}, f32[32,5,8,128]{3,2,1,0:T(8,128)S(1)}, u32[]{:S(2)}, u32[]{:S(2)}) collective-permute-start(f32[32,5,8,128]{3,2,1,0:T(8,128)S(1)} %get-tuple-element.10), channel_id=1, source_target_pairs={{0,24},{8,0},{16,8},{24,16},{1,25},{9,1},{17,9},{25,17},{2,26},{10... | collective-permute-start | bytes 1966088 | tf_op jit(solution)/shard_map/ppermute | solution.py:228
  6.2 0.0 copy-start.3
  6.2 0.8 %edges.1 = (f32[8,2048]{1,0:T(8,128)S(1)}, f32[8,2048]{1,0:T(8,128)S(1)}) custom-call(f32[32,8,8,128]{3,2,1,0:T(8,128)S(1)} %copy-done), custom_call_target="tpu_custom_call" | custom-call | flops 1048576 | bytes 1048576 | tf_op jit(solution)/shard_map/edges/pallas_call | solution.py:231
  7.0 0.0 copy-start.2
  7.0 1.6 %collective-permute-start.2 = (f32[8,2048]{1,0:T(8,128)S(1)}, f32[8,2048]{1,0:T(8,128)S(1)}, u32[]{:S(2)}, u32[]{:S(2)}) collective-permute-start(f32[8,2048]{1,0:T(8,128)S(1)} %get-tuple-element.11), channel_id=1, source_target_pairs={{0,1},{1,2},{2,3},{3,0},{4,5},{5,6},{6,7},{7,4},{8,9},{9,10},{10,1... | collective-permute-start | bytes 196616 | tf_op jit(solution)/shard_map/ppermute | solution.py:232
  8.6 2.2 %collective-permute-start.3 = (f32[8,2048]{1,0:T(8,128)S(1)}, f32[8,2048]{1,0:T(8,128)S(1)}, u32[]{:S(2)}, u32[]{:S(2)}) collective-permute-start(f32[8,2048]{1,0:T(8,128)S(1)} %get-tuple-element.12), channel_id=1, source_target_pairs={{0,3},{1,0},{2,1},{3,2},{4,7},{5,4},{6,5},{7,6},{8,11},{9,8},{10,9... | collective-permute-start | bytes 196616 | tf_op jit(solution)/shard_map/ppermute | solution.py:233
  10.9 0.0 copy-done.3
  10.9 2.5 %collective-permute-done.2.low_ref = f32[8,2048]{1,0:T(8,128)S(1)} collective-permute-done((f32[8,2048]{1,0:T(8,128)S(1)}, f32[8,2048]{1,0:T(8,128)S(1)}, u32[]{:S(2)}, u32[]{:S(2)}) %collective-permute-start.2) | collective-permute-done | bytes 65568 | tf_op jit(solution)/shard_map/ppermute | solution.py:232
  13.4 0.2 collective-permute-done.3.high_ref
  13.6 0.1 broadcast_in_dim.2.scale_ref
  13.7 0.0 copy-done.1
  13.7 0.0 copy-done.2
  13.7 2.0 %inner.1.partial_ref = f32[32,8,8,128]{3,2,1,0:T(8,128)S(1)} custom-call(f32[32,128]{1,0:T(8,128)S(1)} %broadcast_in_dim.2.scale_ref, bf16[384,128]{1,0:T(8,128)(2,1)S(1)} %copy-done.1, bf16[48,128]{1,0:T(8,128)(2,1)S(1)} %copy-done.2, f32[32,8,8,128]{3,2,1,0:T(8,128)S(1)} %copy-done, f32[8,2048]{1,0:T(8,128)S(1)} %collective-permute-done.2.low_ref, ...), custom_call_target="tpu_custom_call" | custom-call | flops 20971520 | bytes 1048576 | tf_op jit(solution)/shard_map/inner/pallas_call | solution.py:246
  15.7 4.0 %collective-permute-done.before_ref = f32[32,5,8,128]{3,2,1,0:T(8,128)S(1)} collective-permute-done((f32[32,5,8,128]{3,2,1,0:T(8,128)S(1)}, f32[32,5,8,128]{3,2,1,0:T(8,128)S(1)}, u32[]{:S(2)}, u32[]{:S(2)}) %collective-permute-start) | collective-permute-done | bytes 655392 | tf_op jit(solution)/shard_map/ppermute | solution.py:227
  19.7 0.8 %collective-permute-done.1.after_ref = f32[32,5,8,128]{3,2,1,0:T(8,128)S(1)} collective-permute-done((f32[32,5,8,128]{3,2,1,0:T(8,128)S(1)}, f32[32,5,8,128]{3,2,1,0:T(8,128)S(1)}, u32[]{:S(2)}, u32[]{:S(2)}) %collective-permute-start.1) | collective-permute-done | bytes 655392 | tf_op jit(solution)/shard_map/ppermute | solution.py:228
  20.5 1.1 %cross.1.partial_ref = f32[32,8,8,128]{3,2,1,0:T(8,128)S(1)} custom-call(f32[32,128]{1,0:T(8,128)S(1)} %broadcast_in_dim.2.scale_ref, f32[32,8,8,128]{3,2,1,0:T(8,128)S(1)} %copy-done, f32[32,5,8,128]{3,2,1,0:T(8,128)S(1)} %collective-permute-done.before_ref, f32[32,5,8,128]{3,2,1,0:T(8,128)S(1)} %collective-permute-done.1.after_ref, ...), custom_call_target="tpu_custom_call", output_to_operand_aliasing={{}: (4, {})} | custom-call | flops 5242880 | bytes 1048576 | tf_op jit(solution)/shard_map/cross/pallas_call | solution.py:247
  21.6 4.8 %collective-permute-done.4.refs_0_ = f32[32,8,8,128]{3,2,1,0:T(8,128)S(1)} collective-permute-done((f32[32,8,8,128]{3,2,1,0:T(8,128)}, f32[32,8,8,128]{3,2,1,0:T(8,128)S(1)}, u32[]{:S(2)}, u32[]{:S(2)}) %collective-permute-start.4) | collective-permute-done | bytes 1048608 | tf_op jit(solution)/shard_map/ppermute | solution.py:214
  26.4 1.3 %outer.1 = f32[32,8,8,128]{3,2,1,0:T(8,128)} custom-call(f32[32,128]{1,0:T(8,128)S(1)} %broadcast_in_dim.2.scale_ref, f32[32,8,8,128]{3,2,1,0:T(8,128)S(1)} %cross.1.partial_ref, f32[32,8,8,128]{3,2,1,0:T(8,128)S(1)} %collective-permute-done.4.refs_0_), custom_call_target="tpu_custom_call" | custom-call | flops 5242880 | bytes 1048576 | tf_op jit(solution)/shard_map/outer/pallas_call | solution.py:252
  (1 shorter events, 0.0 us)
Async XLA Ops:
  0.0 26.4 %collective-permute-start.4 = (f32[32,8,8,128]{3,2,1,0:T(8,128)}, f32[32,8,8,128]{3,2,1,0:T(8,128)S(1)}, u32[]{:S(2)}, u32[]{:S(2)}) collective-permute-start(f32[32,8,8,128]{3,2,1,0:T(8,128)} %u_ref.7), channel_id=1, source_target_pairs={{0,4},{4,0},{1,5},{5,1},{2,6},{6,2},{3,7},{7,3},{8,12},{12,8},{9,1... | collective-permute-start | bytes 3145736 | tf_op jit(solution)/shard_map/ppermute | solution.py:214
  3.0 1.3 %copy-start = (f32[32,8,8,128]{3,2,1,0:T(8,128)S(1)}, f32[32,8,8,128]{3,2,1,0:T(8,128)}, u32[]{:S(2)}) copy-start(f32[32,8,8,128]{3,2,1,0:T(8,128)} %u_ref.7) | copy-start | bytes 3145732
  4.4 15.3 %collective-permute-start = (f32[32,5,8,128]{3,2,1,0:T(8,128)S(1)}, f32[32,5,8,128]{3,2,1,0:T(8,128)S(1)}, u32[]{:S(2)}, u32[]{:S(2)}) collective-permute-start(f32[32,5,8,128]{3,2,1,0:T(8,128)S(1)} %get-tuple-element.9), channel_id=1, source_target_pairs={{0,8},{8,16},{16,24},{24,0},{1,9},{9,17},{17,25},{25,1},{2,10},{10... | collective-permute-start | bytes 1966088 | tf_op jit(solution)/shard_map/ppermute | solution.py:227
  4.5 9.2 %copy-start.1 = (bf16[384,128]{1,0:T(8,128)(2,1)S(1)}, bf16[384,128]{1,0:T(8,128)(2,1)}, u32[]{:S(2)}) copy-start(bf16[384,128]{1,0:T(8,128)(2,1)} %constant.8.clone.band_ref) | copy-start | bytes 294916
  4.5 16.0 %collective-permute-start.1 = (f32[32,5,8,128]{3,2,1,0:T(8,128)S(1)}, f32[32,5,8,128]{3,2,1,0:T(8,128)S(1)}, u32[]{:S(2)}, u32[]{:S(2)}) collective-permute-start(f32[32,5,8,128]{3,2,1,0:T(8,128)S(1)} %get-tuple-element.10), channel_id=1, source_target_pairs={{0,24},{8,0},{16,8},{24,16},{1,25},{9,1},{17,9},{25,17},{2,26},{10... | collective-permute-start | bytes 1966088 | tf_op jit(solution)/shard_map/ppermute | solution.py:228
  6.2 4.7 %copy-start.3 = (f32[32]{0:T(128)S(1)}, f32[32]{0:T(128)}, u32[]{:S(2)}) copy-start(f32[32]{0:T(128)} %param.5) | copy-start | bytes 388
  7.0 6.7 %copy-start.2 = (bf16[48,128]{1,0:T(8,128)(2,1)S(1)}, bf16[48,128]{1,0:T(8,128)(2,1)}, u32[]{:S(2)}) copy-start(bf16[48,128]{1,0:T(8,128)(2,1)} %constant.7.clone.rim_ref) | copy-start | bytes 36868
  7.0 6.4 %collective-permute-start.2 = (f32[8,2048]{1,0:T(8,128)S(1)}, f32[8,2048]{1,0:T(8,128)S(1)}, u32[]{:S(2)}, u32[]{:S(2)}) collective-permute-start(f32[8,2048]{1,0:T(8,128)S(1)} %get-tuple-element.11), channel_id=1, source_target_pairs={{0,1},{1,2},{2,3},{3,0},{4,5},{5,6},{6,7},{7,4},{8,9},{9,10},{10,1... | collective-permute-start | bytes 196616 | tf_op jit(solution)/shard_map/ppermute | solution.py:232
  8.6 5.0 %collective-permute-start.3 = (f32[8,2048]{1,0:T(8,128)S(1)}, f32[8,2048]{1,0:T(8,128)S(1)}, u32[]{:S(2)}, u32[]{:S(2)}) collective-permute-start(f32[8,2048]{1,0:T(8,128)S(1)} %get-tuple-element.12), channel_id=1, source_target_pairs={{0,3},{1,0},{2,1},{3,2},{4,7},{5,4},{6,5},{7,6},{8,11},{9,8},{10,9... | collective-permute-start | bytes 196616 | tf_op jit(solution)/shard_map/ppermute | solution.py:233
